TPU v7x, 128 devices: a whole 4x4x4 slice. The times are simulated.
128 devices in a mesh: rows: 128 (over y, z, x, core).
Axes of the slice: x: 4, y: 4, z: 4, core: 2. Of those that a mesh axis runs over, the one named last changes fastest.
Arguments:
- right_sides: float32 [32, 131072], P(None, 'rows'), may hold values from -48 to 48
- initial: float32 [32, 131072], P(None, 'rows'), may hold values from -1.2 to 1.2
- diag_blocks: float32 [131072, 256], P('rows'), may hold values from -2 to 9
- sub_blocks: float32 [131072, 256], P('rows'), may hold values from -0.21875 to 0.21875
- super_blocks: float32 [131072, 256], P('rows'), may hold values from -0.21875 to 0.21875
- local_inverse: bfloat16 [131072, 1024], P('rows'), may hold values from -1 to 1
- upper_spikes: bfloat16 [256, 131072], P(None, 'rows'), may hold values from -0.21875 to 0.21875
- lower_spikes: bfloat16 [256, 131072], P(None, 'rows'), may hold values from -2 to 2
Outputs:
- solution: float32 [32, 131072], P(None, 'rows')
- residual_norms: float32 [3, 32], replicated
All inputs are finite; a program needn't handle non-finite values.
Results may differ from a plain program's by a relative error of at most 0.002.
The roundings to bfloat16 on the way count: a program that leaves them out, or rounds other values in their place, can miss the bound.
Values may be sent and summed in bfloat16 or wider, within the bound.
A program may use at most 64 MiB of HBM per device.

v0:
```python
import functools

import jax
import jax.numpy as jnp
from jax import lax
from jax.sharding import Mesh
from jax.sharding import PartitionSpec as P

ITERS = 2
ROWS = ("rows_0", "rows_1", "rows_2", "rows_3")


maximum_level = lax.Precision.HIGHEST


def with_halo(block, sides, width):
    for axis, dim in sides:
        count = lax.axis_size(axis)
        forward = [(i, i + 1) for i in range(count - 1)]
        backward = [(target, source) for source, target in forward]
        low = lax.ppermute(
            lax.slice_in_dim(block, block.shape[dim] - width, None, axis=dim), axis, forward
        )
        high = lax.ppermute(lax.slice_in_dim(block, 0, width, axis=dim), axis, backward)
        block = jnp.concatenate([low, block, high], axis=dim)
    return block


def shifted(block, axis, distance):
    devices = range(lax.axis_size(axis))
    route = [(i - distance, i) for i in devices if i - distance in devices]
    return lax.ppermute(block, axis, route)


def one_axis_at_a_time(value, axes):
    return functools.reduce(lax.psum, axes, value)


def filled_with(value, identity):
    return jax.tree.map(
        lambda a, e: jnp.broadcast_to(jnp.asarray(e, a.dtype), a.shape), value, identity
    )


def prefix_by_axis(value, axes, combine, identity):
    before = start = filled_with(value, identity)
    running = value
    for axis in reversed(axes):
        count, index = (lax.axis_size(axis), lax.axis_index(axis))
        pieces = jax.tree.map(lambda part: lax.all_gather(part, axis), running)
        inside, running = (start, start)
        for k in range(count):
            passed = k < index
            running = combine(running, jax.tree.map(lambda part: part[k], pieces))
            inside = jax.tree.map(lambda new, old: jnp.where(passed, new, old), running, inside)
        before = combine(inside, before)
    return before


def split_blocks(matrix, band_width):
    return matrix.reshape(matrix.shape[0] // band_width, band_width, band_width)


def residual_of(right_sides, solution, diag_mat, lower_mat, upper_mat, band_width):
    padded = with_halo(solution, ((ROWS, 1),), band_width)
    block_count = diag_mat.shape[0]
    stacked = padded.reshape(padded.shape[0], block_count + 2, band_width)
    applied = jnp.einsum("rkb,kbc->rkc", stacked[:, 1:-1], diag_mat, precision=maximum_level)
    applied = applied + jnp.einsum(
        "rkb,kbc->rkc", stacked[:, :-2], lower_mat, precision=maximum_level
    )
    applied = applied + jnp.einsum(
        "rkb,kbc->rkc", stacked[:, 2:], upper_mat, precision=maximum_level
    )
    return right_sides - applied.reshape(right_sides.shape)


def compose(earlier, successor_block):
    matrices = jnp.matmul(earlier[0], successor_block[0], precision=maximum_level)
    sums = jnp.matmul(earlier[1], successor_block[0], precision=maximum_level) + successor_block[1]
    return (matrices, sums)


def body(
    right_sides,
    initial,
    diag_blocks,
    sub_blocks,
    super_blocks,
    local_inverse,
    upper_spikes,
    lower_spikes,
):
    band_width = diag_blocks.shape[1]
    diag_mat = split_blocks(diag_blocks, band_width)
    lower_mat = split_blocks(sub_blocks, band_width)
    upper_mat = split_blocks(super_blocks, band_width)
    chain_mat = -lower_spikes[:, -band_width:].astype(jnp.float32)
    bottom_upper = upper_spikes[:, -band_width:].astype(jnp.float32)
    order_total = right_sides.shape[1] * lax.axis_size(ROWS)
    next_lower = shifted(lower_spikes[:, :band_width], ROWS, -1).astype(jnp.float32)
    records = []

    def record_norm(residual):
        partial_sum = jnp.sum(residual * residual, axis=1)
        records.append(one_axis_at_a_time(partial_sum, ROWS))

    solution = initial
    for turn_index in range(ITERS):
        residual = residual_of(right_sides, solution, diag_mat, lower_mat, upper_mat, band_width)
        record_norm(residual)
        rounded = residual.astype(jnp.bfloat16)
        local_part = jnp.dot(rounded, local_inverse, preferred_element_type=jnp.float32)
        own_top = local_part[:, :band_width]
        next_top = shifted(own_top, ROWS, -1)
        offset = local_part[:, -band_width:] - jnp.matmul(
            next_top, bottom_upper, precision=maximum_level
        )
        identity = (jnp.eye(band_width, dtype=jnp.float32), jnp.zeros_like(offset))
        leading_portion = prefix_by_axis((chain_mat, offset), ROWS, compose, identity)
        previous = leading_portion[1]
        current = offset + jnp.matmul(previous, chain_mat, precision=maximum_level)
        top_tip = next_top - jnp.matmul(current, next_lower, precision=maximum_level)
        correction = local_part - jnp.dot(
            top_tip.astype(jnp.bfloat16), upper_spikes, preferred_element_type=jnp.float32
        )
        correction = correction - jnp.dot(
            previous.astype(jnp.bfloat16), lower_spikes, preferred_element_type=jnp.float32
        )
        solution = solution + correction
    residual = residual_of(right_sides, solution, diag_mat, lower_mat, upper_mat, band_width)
    record_norm(residual)
    totals = jnp.stack(records)
    return (solution, jnp.sqrt(totals / order_total))


def solution(mesh):
    finer = Mesh(mesh.devices.reshape(4, 4, 4, 2), ("rows_0", "rows_1", "rows_2", "rows_3"))
    placed = (
        P(None, ROWS),
        P(None, ROWS),
        P(ROWS, None),
        P(ROWS, None),
        P(ROWS, None),
        P(ROWS, None),
        P(None, ROWS),
        P(None, ROWS),
    )
    return jax.shard_map(
        body, mesh=finer, in_specs=placed, out_specs=(P(None, ROWS), P()), check_vma=False
    )
```

profile of v0, /device:TPU:0, one launch (start us, length us, event | category | flops | bytes accessed | tf_op | source)
XLA Modules:
  0.0 258.3 jit_solution(14841038663907995884)
XLA Ops:
  8.8 2.0 collective-permute-start
  15.9 4.8 %all-gather = f32[512,256]{1,0:T(8,128)S(1)} all-gather(f32[256,256]{1,0:T(8,128)S(1)} %convert_negate_fusion), channel_id=2, replica_groups=mesh['rows_0'=4,'rows_1'=4,'rows_2'=4,'rows_3'=2] {'rows_3'}, dimensions={0}, use_global_device_ids=true | all-gather | bytes 786432 | tf_op jit(solution)/shard_map/all_gather | solution.py:50
  23.7 1.8 fusion.44
  27.0 1.7 reshape.31
  34.8 16.0 %all-gather.16.cloned.1.call-done = f32[1024,256]{1,0:T(8,128)} async-done(((f32[256,256]{1,0:T(8,128)}), f32[1024,256]{1,0:T(8,128)}) %all-gather.16.cloned.1.call-update) | async-done | bytes 1048592 | tf_op jit(solution)/shard_map/all_gather | solution.py:50
  56.8 2.0 fusion.59
  60.2 1.9 all-gather.4
  63.9 12.0 %all-gather.5 = f32[128,256]{1,0:T(8,128)S(1)} all-gather(f32[32,256]{1,0:T(8,128)S(1)} %slice_add_fusion.8), channel_id=7, replica_groups=mesh['rows_0'=4,'rows_1'=4,'rows_2'=4,'rows_3'=2] {'rows_2'}, dimensions={0}, use_global_device_ids=true | all-gather | bytes 163840 | tf_op jit(solution)/shard_map/all_gather | solution.py:50
  80.8 1.8 convolution_add_fusion.25
  89.8 2.0 fusion.47
  92.0 1.7 fusion.120
  93.7 12.7 %all-gather.6 = f32[128,256]{1,0:T(8,128)S(1)} all-gather(f32[32,256]{1,0:T(8,128)} %convolution_add_fusion.25), channel_id=8, replica_groups=mesh['rows_0'=4,'rows_1'=4,'rows_2'=4,'rows_3'=2] {'rows_1'}, dimensions={0}, use_global_device_ids=true | all-gather | bytes 163840 | tf_op jit(solution)/shard_map/all_gather | solution.py:50
  111.2 13.2 %all-gather.7 = f32[128,256]{1,0:T(8,128)} all-gather(f32[32,256]{1,0:T(8,128)S(1)} %convolution_add_fusion.22), channel_id=9, replica_groups=mesh['rows_0'=4,'rows_1'=4,'rows_2'=4,'rows_3'=2] {'rows_0'}, dimensions={0}, use_global_device_ids=true | all-gather | bytes 163840 | tf_op jit(solution)/shard_map/all_gather | solution.py:50
  139.1 2.7 %collective-permute-done.5 = f32[32,256]{1,0:T(8,128)S(1)} collective-permute-done((f32[32,256]{1,0:T(8,128)S(1)}, f32[32,256]{1,0:T(8,128)S(1)}, u32[]{:S(2)}, u32[]{:S(2)}) %collective-permute-start.5) | collective-permute-done | bytes 32800 | tf_op jit(solution)/shard_map/ppermute | solution.py:24
  149.9 3.9 %collective-permute-done.6 = f32[32,256]{1,0:T(8,128)S(1)} collective-permute-done((f32[32,256]{1,0:T(8,128)S(1)}, f32[32,256]{1,0:T(8,128)S(1)}, u32[]{:S(2)}, u32[]{:S(2)}) %collective-permute-start.6) | collective-permute-done | bytes 32800 | tf_op jit(solution)/shard_map/ppermute | solution.py:32
  154.0 4.1 %all-gather.8 = f32[64,256]{1,0:T(8,128)S(1)} all-gather(f32[32,256]{1,0:T(8,128)S(1)} %convolution_subtract_fusion.5), channel_id=10, replica_groups=mesh['rows_0'=4,'rows_1'=4,'rows_2'=4,'rows_3'=2] {'rows_3'}, dimensions={0}, use_global_device_ids=true | all-gather | bytes 98304 | tf_op jit(solution)/shard_map/all_gather | solution.py:50
  158.4 16.1 %all-gather.9 = f32[128,256]{1,0:T(8,128)S(1)} all-gather(f32[32,256]{1,0:T(8,128)S(1)} %slice_add_fusion.3), channel_id=11, replica_groups=mesh['rows_0'=4,'rows_1'=4,'rows_2'=4,'rows_3'=2] {'rows_2'}, dimensions={0}, use_global_device_ids=true | all-gather | bytes 163840 | tf_op jit(solution)/shard_map/all_gather | solution.py:50
  175.5 15.6 %all-gather.10 = f32[128,256]{1,0:T(8,128)S(1)} all-gather(f32[32,256]{1,0:T(8,128)S(1)} %convolution_add_fusion.14), channel_id=12, replica_groups=mesh['rows_0'=4,'rows_1'=4,'rows_2'=4,'rows_3'=2] {'rows_1'}, dimensions={0}, use_global_device_ids=true | all-gather | bytes 163840 | tf_op jit(solution)/shard_map/all_gather | solution.py:50
  192.1 12.0 %all-gather.11 = f32[128,256]{1,0:T(8,128)S(1)} all-gather(f32[32,256]{1,0:T(8,128)S(1)} %convolution_add_fusion.11), channel_id=13, replica_groups=mesh['rows_0'=4,'rows_1'=4,'rows_2'=4,'rows_3'=2] {'rows_0'}, dimensions={0}, use_global_device_ids=true | all-gather | bytes 163840 | tf_op jit(solution)/shard_map/all_gather | solution.py:50
  209.7 4.0 %collective-permute-done.8 = f32[32,256]{1,0:T(8,128)S(1)} collective-permute-done((f32[32,256]{1,0:T(8,128)S(1)}, f32[32,256]{1,0:T(8,128)S(1)}, u32[]{:S(2)}, u32[]{:S(2)}) %collective-permute-start.8) | collective-permute-done | bytes 32800 | tf_op jit(solution)/shard_map/ppermute | solution.py:24
  218.3 15.0 %all-reduce.2 = (f32[32]{0:T(128)S(1)}, f32[32]{0:T(128)S(1)}, f32[32]{0:T(128)S(1)}) all-reduce(f32[32]{0:T(128)S(1)} %get-tuple-element.4, f32[32]{0:T(128)S(1)} %get-tuple-element.3, f32[32]{0:T(128)S(1)} %get-tuple-element.2), channel_id=1, replica_groups=mesh['rows_0'=4,'rows_1'=4,'rows_2'=4,'rows_3'=2] {'rows_0'}, use_global_device_ids=true, to_apply=%region_11.12 | all-reduce | flops 96 | bytes 768 | tf_op jit(solution)/shard_map/psum | solution.py:36
  233.3 7.7 %all-reduce.1 = (f32[32]{0:T(128)S(1)}, f32[32]{0:T(128)S(1)}, f32[32]{0:T(128)S(1)}) all-reduce(f32[32]{0:T(128)S(1)} %get-tuple-element.11, f32[32]{0:T(128)S(1)} %get-tuple-element.12, f32[32]{0:T(128)S(1)} %get-tuple-element.13), channel_id=1, replica_groups=mesh['rows_0'=4,'rows_1'=4,'rows_2'=4,'rows_3'=2] {'rows_1'}, use_global_device_ids=true, to_apply=%region_12.13 | all-reduce | flops 96 | bytes 768 | tf_op jit(solution)/shard_map/psum | solution.py:36
  241.0 7.7 %all-reduce = (f32[32]{0:T(128)S(1)}, f32[32]{0:T(128)S(1)}, f32[32]{0:T(128)S(1)}) all-reduce(f32[32]{0:T(128)S(1)} %get-tuple-element.8, f32[32]{0:T(128)S(1)} %get-tuple-element.9, f32[32]{0:T(128)S(1)} %get-tuple-element.10), channel_id=1, replica_groups=mesh['rows_0'=4,'rows_1'=4,'rows_2'=4,'rows_3'=2] {'rows_2'}, use_global_device_ids=true, to_apply=%region_13.14 | all-reduce | flops 96 | bytes 768 | tf_op jit(solution)/shard_map/psum | solution.py:36
  248.8 2.5 all-reduce.3
  (219 shorter events, 78.5 us)
Async XLA Ops:
  7.2 43.6 %all-gather.16.cloned.1.call-start = ((), (), s32[]{:S(2)}) async-start(), calls=%async_computation | async-start | bytes 1310720 | tf_op jit(solution)/shard_map/all_gather | solution.py:50
  8.8 16.7 %collective-permute-start = (f32[32,256]{1,0:T(8,128)}, f32[32,256]{1,0:T(8,128)}, u32[]{:S(2)}, u32[]{:S(2)}) collective-permute-start(f32[32,256]{1,0:T(8,128)} %get-tuple-element.30), channel_id=1, source_target_pairs={{0,1},{1,2},{2,3},{3,4},{4,5},{5,6},{6,7},{7,8},{8,9},{9,10},{10,1... | collective-permute-start | bytes 98312 | tf_op jit(solution)/shard_map/ppermute | solution.py:21
  10.8 14.7 %collective-permute-start.1 = (f32[32,256]{1,0:T(8,128)}, f32[32,256]{1,0:T(8,128)}, u32[]{:S(2)}, u32[]{:S(2)}) collective-permute-start(f32[32,256]{1,0:T(8,128)} %get-tuple-element.31), channel_id=1, source_target_pairs={{1,0},{2,1},{3,2},{4,3},{5,4},{6,5},{7,6},{8,7},{9,8},{10,9},{11,1... | collective-permute-start | bytes 98312 | tf_op jit(solution)/shard_map/ppermute | solution.py:24
  13.7 121.0 %collective-permute-start.3 = (bf16[256,256]{1,0:T(8,128)(2,1)}, bf16[256,256]{1,0:T(8,128)(2,1)}, u32[]{:S(2)}, u32[]{:S(2)}) collective-permute-start(bf16[256,256]{1,0:T(8,128)(2,1)} %slice.243), channel_id=1, source_target_pairs={{1,0},{2,1},{3,2},{4,3},{5,4},{6,5},{7,6},{8,7},{9,8},{10,9},{11,1... | collective-permute-start | bytes 393224 | tf_op jit(solution)/shard_map/ppermute | solution.py:32
  23.3 60.5 %all-gather.18.cloned.1.call-start = ((), (), s32[]{:S(2)}) async-start(), calls=%async_computation.1 | async-start | bytes 1310720 | tf_op jit(solution)/shard_map/all_gather | solution.py:50
  33.5 25.4 %collective-permute-start.2 = (f32[32,256]{1,0:T(8,128)}, f32[32,256]{1,0:T(8,128)}, u32[]{:S(2)}, u32[]{:S(2)}) collective-permute-start(f32[32,256]{1,0:T(8,128)} %slice.315), channel_id=1, source_target_pairs={{1,0},{2,1},{3,2},{4,3},{5,4},{6,5},{7,6},{8,7},{9,8},{10,9},{11,1... | collective-permute-start | bytes 98312 | tf_op jit(solution)/shard_map/ppermute | solution.py:32
  58.9 67.5 %all-gather.20.cloned.1.call-start = ((), (), s32[]{:S(2)}) async-start(), calls=%async_computation.2 | async-start | bytes 1310720 | tf_op jit(solution)/shard_map/all_gather | solution.py:50
  91.9 32.5 %copy-start.14 = (f32[256,256]{1,0:T(8,128)S(1)}, f32[256,256]{1,0:T(8,128)}, u32[]{:S(2)}) copy-start(f32[256,256]{1,0:T(8,128)} %fusion.21) | copy-start | bytes 786436
  91.9 33.3 %copy-start.20 = (f32[256,256]{1,0:T(8,128)S(1)}, f32[256,256]{1,0:T(8,128)}, u32[]{:S(2)}) copy-start(f32[256,256]{1,0:T(8,128)} %copy-done.19) | copy-start | bytes 786436
  91.9 33.3 %copy-start.22 = (f32[256,256]{1,0:T(8,128)S(1)}, f32[256,256]{1,0:T(8,128)}, u32[]{:S(2)}) copy-start(f32[256,256]{1,0:T(8,128)} %copy-done.21) | copy-start | bytes 786436
  91.9 33.3 %copy-start.30 = (f32[256,256]{1,0:T(8,128)S(1)}, f32[256,256]{1,0:T(8,128)}, u32[]{:S(2)}) copy-start(f32[256,256]{1,0:T(8,128)} %copy-done.29) | copy-start | bytes 786436
  91.9 33.3 %copy-start.31 = (f32[256,256]{1,0:T(8,128)S(1)}, f32[256,256]{1,0:T(8,128)}, u32[]{:S(2)}) copy-start(f32[256,256]{1,0:T(8,128)} %fusion.47) | copy-start | bytes 786436
  136.3 2.8 %collective-permute-start.4 = (f32[32,256]{1,0:T(8,128)S(1)}, f32[32,256]{1,0:T(8,128)S(1)}, u32[]{:S(2)}, u32[]{:S(2)}) collective-permute-start(f32[32,256]{1,0:T(8,128)S(1)} %get-tuple-element.28), channel_id=1, source_target_pairs={{0,1},{1,2},{2,3},{3,4},{4,5},{5,6},{6,7},{7,8},{8,9},{9,10},{10,1... | collective-permute-start | bytes 98312 | tf_op jit(solution)/shard_map/ppermute | solution.py:21
  137.6 4.2 %collective-permute-start.5 = (f32[32,256]{1,0:T(8,128)S(1)}, f32[32,256]{1,0:T(8,128)S(1)}, u32[]{:S(2)}, u32[]{:S(2)}) collective-permute-start(f32[32,256]{1,0:T(8,128)S(1)} %get-tuple-element.29), channel_id=1, source_target_pairs={{1,0},{2,1},{3,2},{4,3},{5,4},{6,5},{7,6},{8,7},{9,8},{10,9},{11,1... | collective-permute-start | bytes 98312 | tf_op jit(solution)/shard_map/ppermute | solution.py:24
  147.8 43.3 %copy-start.9 = (f32[1024,256]{1,0:T(8,128)S(1)}, f32[1024,256]{1,0:T(8,128)}, u32[]{:S(2)}) copy-start(f32[1024,256]{1,0:T(8,128)} %all-gather.18.cloned.1.call-done) | copy-start | bytes 3145732
  147.8 43.3 %copy-start.45 = (f32[32,256]{1,0:T(8,128)S(1)}, f32[32,256]{1,0:T(8,128)}, u32[]{:S(2)}) copy-start(f32[32,256]{1,0:T(8,128)} %copy-done.44) | copy-start | bytes 98308
  148.4 43.4 %copy-start.15 = (f32[256,256]{1,0:T(8,128)S(1)}, f32[256,256]{1,0:T(8,128)}, u32[]{:S(2)}) copy-start(f32[256,256]{1,0:T(8,128)} %fusion.21) | copy-start | bytes 786436
  148.4 55.7 %copy-start.18 = (f32[1024,256]{1,0:T(8,128)S(1)}, f32[1024,256]{1,0:T(8,128)}, u32[]{:S(2)}) copy-start(f32[1024,256]{1,0:T(8,128)} %all-gather.20.cloned.1.call-done) | copy-start | bytes 3145732
  148.5 55.7 %copy-start.51 = (f32[32,256]{1,0:T(8,128)S(1)}, f32[32,256]{1,0:T(8,128)}, u32[]{:S(2)}) copy-start(f32[32,256]{1,0:T(8,128)} %copy-done.50) | copy-start | bytes 98308
  148.5 5.4 %collective-permute-start.6 = (f32[32,256]{1,0:T(8,128)S(1)}, f32[32,256]{1,0:T(8,128)S(1)}, u32[]{:S(2)}, u32[]{:S(2)}) collective-permute-start(f32[32,256]{1,0:T(8,128)S(1)} %slice.350), channel_id=1, source_target_pairs={{1,0},{2,1},{3,2},{4,3},{5,4},{6,5},{7,6},{8,7},{9,8},{10,9},{11,1... | collective-permute-start | bytes 98312 | tf_op jit(solution)/shard_map/ppermute | solution.py:32
  174.8 30.1 %copy-start.28 = (f32[256,256]{1,0:T(8,128)S(1)}, f32[256,256]{1,0:T(8,128)}, u32[]{:S(2)}) copy-start(f32[256,256]{1,0:T(8,128)} %fusion.16) | copy-start | bytes 786436
  175.3 30.0 %copy-start.13 = (bf16[256,1024]{1,0:T(8,128)(2,1)S(1)}, bf16[256,1024]{1,0:T(8,128)(2,1)}, u32[]{:S(2)}) copy-start(bf16[256,1024]{1,0:T(8,128)(2,1)} %param.15) | copy-start | bytes 1572868
  207.1 2.6 %collective-permute-start.7 = (f32[32,256]{1,0:T(8,128)S(1)}, f32[32,256]{1,0:T(8,128)S(1)}, u32[]{:S(2)}, u32[]{:S(2)}) collective-permute-start(f32[32,256]{1,0:T(8,128)S(1)} %get-tuple-element.26), channel_id=1, source_target_pairs={{0,1},{1,2},{2,3},{3,4},{4,5},{5,6},{6,7},{7,8},{8,9},{9,10},{10,1... | collective-permute-start | bytes 98312 | tf_op jit(solution)/shard_map/ppermute | solution.py:21
  208.4 5.3 %collective-permute-start.8 = (f32[32,256]{1,0:T(8,128)S(1)}, f32[32,256]{1,0:T(8,128)S(1)}, u32[]{:S(2)}, u32[]{:S(2)}) collective-permute-start(f32[32,256]{1,0:T(8,128)S(1)} %get-tuple-element.27), channel_id=1, source_target_pairs={{1,0},{2,1},{3,2},{4,3},{5,4},{6,5},{7,6},{8,7},{9,8},{10,9},{11,1... | collective-permute-start | bytes 98312 | tf_op jit(solution)/shard_map/ppermute | solution.py:24
  (46 other events, 347.8 us)
Sparse Core Ops, SparseCore 0:
  23.4 27.3 all-gather.15
  59.0 24.6 all-gather.17
  92.0 24.5 all-gather.19
where the time goes:
time: 261 us; the launch traced here: 258 us
  blocking collectives  125 us (48%)
  matrix products  55.2 us (21%)
  waiting for transfers between devices  26.6 us (10%)
  local copies, waits for them, and re-layouts  19 us (7%)
  between operations  14.9 us (6%)
  starting transfers between devices  12.8 us (5%)
  other arithmetic  4.58 us (2%)
    all_gather x9, blocking collectives, prefix_by_axis(): pieces = jax.tree.map(lambda part: lax.all_gather(part, axis), running)  92.3 us
    psum x4, blocking collectives, one_axis_at_a_time(): return functools.reduce(lax.psum, axes, value)  32.9 us
    dot_general x32, matrix products, compose(): jnp.matmul(earlier[1], successor_block[0], precision=maximum_level)  26.2 us
    all_gather x3, waiting for transfers between devices, prefix_by_axis(): pieces = jax.tree.map(lambda part: lax.all_gather(part, axis), running)  16 us
    dot_general x13, matrix products, compose(): jnp.matmul(earlier[0], successor_block[0], precision=maximum_level)  15.9 us
    unnamed x116, local copies, waits for them, and re-layouts  8.11 us
    ppermute x3, waiting for transfers between devices, with_halo(): lax.ppermute(lax.slice_in_dim(block, 0, width, axis=dim), axis, backward)  6.69 us
  transfers between devices with their start and end apart: 12, of which 4 were waited for; matrix products, arithmetic and copies ran while one was open for 20% of the time, Pallas kernels for 0%

commit v1 on v0

v1 whole, which is shorter than its diff:
```python
import functools

import jax
import jax.numpy as jnp
from jax import lax
from jax.experimental import pallas as pl
from jax.experimental.pallas import tpu as pltpu
from jax.sharding import PartitionSpec as P

ITERS = 2
BAND = 256
RHS = 32
COLS = 1024
PARTS = 128
ORDER = 131072
COPIES = 64
MESH = pl.DeviceIdType.MESH
F32 = jnp.float32
BF16 = jnp.bfloat16


def rounded(value):
    return value.astype(BF16)


def two_terms(value):
    high = rounded(value)
    return high, rounded(value - high.astype(F32))


def three_terms(value):
    high = rounded(value)
    rest = value - high.astype(F32)
    middle = rounded(rest)
    return high, middle, rounded(rest - middle.astype(F32))


def dot(a, b):
    return jnp.dot(a, b, preferred_element_type=F32)


def times_exact(value, weight):
    rows = value.shape[0]
    out = dot(jnp.concatenate(three_terms(value), axis=0), weight)
    return out[:rows] + (out[rows : 2 * rows] + out[2 * rows :])


def times_pair(value, high, low):
    rows = value.shape[0]
    terms = jnp.concatenate(three_terms(value), axis=0)
    out = dot(terms, high)
    small = dot(terms[: 2 * rows], low)
    rest = (out[rows : 2 * rows] + out[2 * rows :]) + (small[:rows] + small[rows:])
    return out[:rows] + rest


def matrix_times(a, b):
    a_high, a_low = a
    b_high, b_low = b
    size = a_high.shape[0]
    out = dot(jnp.concatenate([a_high, a_low], axis=0), b_high)
    return out[:size] + (out[size:] + dot(a_high, b_low))


def store_halves(ref, slot, matrix):
    high, low = two_terms(matrix)
    half = BAND // 2
    for k in range(2):
        rows = slice(k * half, (k + 1) * half)
        ref[slot, k, :half, :] = high[rows]
        ref[slot, k, half:, :] = low[rows]


def load_halves(ref, slot):
    half = BAND // 2
    high = jnp.concatenate([ref[slot, 0, :half, :], ref[slot, 1, :half, :]], axis=0)
    low = jnp.concatenate([ref[slot, 0, half:, :], ref[slot, 1, half:, :]], axis=0)
    return high, low


def kernel(
    rhs_hbm, x0_hbm, diag_hbm, sub_hbm, sup_hbm, inv_hbm, up_hbm, low_hbm,
    x_out, norm_out,
    rhs, diag, sub, sup, inv, up, low, a_high, a_low,
    xp, pair_mat, up_before, low_after, gx, gz, gy, mpx, mpz,
    local, next_top, vc, vx, vz, vy, prefix, squares, totals,
    load_sem, send_sem, recv_sem,
):
    me = lax.axis_index("rows")
    core = lax.rem(me, 2)
    ix = lax.rem(me // 2, 4)
    iz = lax.rem(me // 8, 4)
    iy = me // 32
    partner = me + 1 - 2 * core

    def on_x(d):
        return me - 2 * ix + 2 * lax.rem(ix + d, 4)

    def on_z(d):
        return me - 8 * iz + 8 * lax.rem(iz + d, 4)

    def on_y(d):
        return me - 32 * iy + 32 * lax.rem(iy + d, 4)

    has_before = me > 0
    has_after = me < PARTS - 1

    barrier = pltpu.get_barrier_semaphore()
    peers = [partner]
    for d in (1, 2, 3):
        peers += [on_x(d), on_z(d), on_y(d)]
    peers += [lax.rem(me + 1, PARTS), lax.rem(me + PARTS - 1, PARTS)]
    for peer in peers:
        pl.semaphore_signal(barrier, inc=1, device_id=(peer,), device_id_type=MESH)

    loads = {}

    def load(name, source, target):
        copy = pltpu.make_async_copy(source, target, load_sem.at[len(loads)])
        copy.start()
        loads[name] = copy

    last = slice(COLS - BAND, COLS)
    load("pair", low_hbm.at[:, last], pair_mat.at[core])
    load("x0", x0_hbm, xp.at[0, :, BAND : BAND + COLS])
    load("up", up_hbm, up)
    load("low", low_hbm, low)
    load("diag", diag_hbm, diag)
    load("sub", sub_hbm, sub)
    load("sup", sup_hbm, sup)
    load("rhs", rhs_hbm, rhs)
    load("inv", inv_hbm, inv)

    @pl.when(jnp.logical_not(has_before))
    def _():
        up_before[...] = jnp.zeros_like(up_before)
        for k in range(ITERS + 1):
            xp[k, :, :BAND] = jnp.zeros((RHS, BAND), F32)

    @pl.when(jnp.logical_not(has_after))
    def _():
        low_after[...] = jnp.zeros_like(low_after)
        for k in range(ITERS + 1):
            xp[k, :, BAND + COLS :] = jnp.zeros((RHS, BAND), F32)
        for k in range(ITERS):
            next_top[k] = jnp.zeros((RHS, BAND), F32)

    pl.semaphore_wait(barrier, len(peers))

    counter = iter(range(COPIES))
    sent = []

    class Copy:
        def __init__(self, source, target, device, sends=None, receives=None):
            i = next(counter)
            self.copy = pltpu.make_async_remote_copy(
                src_ref=source,
                dst_ref=target,
                send_sem=send_sem.at[i],
                recv_sem=recv_sem.at[i],
                device_id=(device,),
                device_id_type=MESH,
            )
            self.sends, self.receives = sends, receives
            sent.append(self)
            self.guard(sends, self.copy.start)

        def guard(self, condition, action):
            if condition is None:
                action()
            else:
                pl.when(condition)(lambda: action())

        def arrived(self):
            self.guard(self.receives, self.copy.wait_recv)

        def left(self):
            self.guard(self.sends, self.copy.wait_send)

    def to_after(source, target):
        return Copy(source, target, lax.rem(me + 1, PARTS), has_after, has_before)

    def to_before(source, target):
        return Copy(source, target, lax.rem(me + PARTS - 1, PARTS), has_before, has_after)

    def send_edges(k):
        return (
            to_after(xp.at[k, :, COLS : COLS + BAND], xp.at[k, :, :BAND]),
            to_before(xp.at[k, :, BAND : 2 * BAND], xp.at[k, :, BAND + COLS :]),
        )

    loads["pair"].wait()
    pair_copy = Copy(pair_mat.at[core], pair_mat.at[core], partner)
    loads["x0"].wait()
    edges = send_edges(0)
    loads["up"].wait()
    up_copy = to_after(up.at[:, last], up_before)
    loads["low"].wait()
    low_copy = to_before(low.at[:, :BAND], low_after)

    pair_copy.arrived()
    store_halves(gx, ix, dot(pair_mat[0], pair_mat[1]))

    def send_matrix(ref, slot, peer_of, senders=None):
        copies = []
        for d in (1, 2, 3):
            sends, receives = (None, None) if senders is None else senders[d]
            if sends is False:
                continue
            copies.append(
                (d, Copy(ref.at[slot, core], ref.at[slot, core], peer_of(d), sends, receives))
            )
        return copies

    def pass_on(ref, slot, copies):
        passed = []
        for d, copy in copies:
            copy.arrived()
            origin = lax.rem(slot + 4 - d, 4)
            passed.append(
                Copy(ref.at[origin, core], ref.at[origin, core], partner, copy.receives, copy.receives)
            )
        for copy in passed:
            copy.arrived()

    def products(ref, out):
        m = [load_halves(ref, q) for q in range(4)]
        two = two_terms(matrix_times(m[0], m[1]))
        other = two_terms(matrix_times(m[2], m[3]))
        total = matrix_times(two, other)
        return m, two, total

    def store_prefixes(out, m, two):
        row = lax.broadcasted_iota(jnp.int32, (BAND, BAND), 0)
        col = lax.broadcasted_iota(jnp.int32, (BAND, BAND), 1)
        unit = (row == col).astype(F32).astype(BF16)
        three = two_terms(matrix_times(two, m[2]))
        for q, (high, low_term) in enumerate(
            [(unit, jnp.zeros_like(unit)), m[0], two, three]
        ):
            out[q, :BAND, :] = high
            out[q, BAND:, :] = low_term

    x_matrices = send_matrix(gx, ix, on_x)

    for name, source, place in (("sub", sub, 0), ("diag", diag, 1), ("sup", sup, 2)):
        loads[name].wait()
        for m in range(4):
            high, low_term = two_terms(source[m * BAND : (m + 1) * BAND, :])
            rows = slice(place * BAND, (place + 1) * BAND)
            a_high[m, rows, :] = high
            a_low[m, rows, :] = low_term
    loads["rhs"].wait()

    def applied(k, m, first, count):
        start = (m + first) * BAND
        value = xp[k, :, start : start + count * BAND]
        rows = slice(first * BAND, (first + count) * BAND)
        return times_pair(value, a_high[m, rows, :], a_low[m, rows, :])

    def residual(k, halos):
        parts = [
            applied(k, 0, 1, 2),
            applied(k, 1, 0, 3),
            applied(k, 2, 0, 3),
            applied(k, 3, 0, 2),
        ]
        for copy in halos:
            copy.arrived()
        parts[0] = parts[0] + applied(k, 0, 0, 1)
        parts[3] = parts[3] + applied(k, 3, 2, 1)
        parts = [rhs[:, m * BAND : (m + 1) * BAND] - parts[m] for m in range(4)]
        total = jnp.zeros((RHS, 128), F32)
        for part in parts:
            total = total + (part[:, :128] * part[:, :128] + part[:, 128:] * part[:, 128:])
        squares[k] = total
        return parts

    def exchange(ref, k, slot, peer_of, conditions=None):
        copies = []
        for d in (1, 2, 3):
            sends, receives = (None, None) if conditions is None else conditions[d]
            copies.append(Copy(ref.at[k, slot], ref.at[k, slot], peer_of(d), sends, receives))
        return copies

    def prefixes(ref, k, matrices, where, slot, total=True):
        running = ref[k, 0]
        prefix[where, 0] = jnp.zeros((RHS, BAND), F32)
        prefix[where, 1] = running
        for q in (1, 2, 3):
            if q == 3 and not total:
                return None
            running = times_pair(running, *matrices(q)) + ref[k, q]
            if q < 3:
                prefix[where, q + 1] = running
        return running

    y_conditions = {d: (iy + d < 4, iy >= d) for d in (1, 2, 3)}
    y_matrix_conditions = {
        1: (jnp.logical_and(iy >= 1, iy <= 2), iy >= 2),
        2: (iy == 1, iy == 3),
        3: (False, False),
    }

    for k in range(ITERS):
        parts = residual(k, edges)
        if k == 0:
            loads["inv"].wait()
        whole = jnp.concatenate([rounded(part) for part in parts], axis=1)
        top_block = dot(whole, inv[:, :BAND])
        local[k, :, :BAND] = top_block
        top_copy = to_before(local.at[k, :, :BAND], next_top.at[k])
        bottom_block = dot(whole, inv[:, last])
        if k == 0:
            up_copy.arrived()
        shift = -times_exact(top_block, up_before[...])
        vc[k, core] = bottom_block - times_exact(shift, pair_mat[core])
        pair_vector = Copy(vc.at[k, core], vc.at[k, core], partner)
        local[k, :, BAND : COLS - BAND] = dot(whole, inv[:, BAND : COLS - BAND])
        pair_vector.arrived()
        vx[k, ix] = vc[k, 1] - times_exact(vc[k, 0], pair_mat[1])
        x_copies = exchange(vx, k, ix, on_x)
        if k == 0:
            pass_on(gx, ix, x_matrices)
            m, two, total = products(gx, mpx)
            store_halves(gz, iz, total)
            z_matrices = send_matrix(gz, iz, on_z)
            store_prefixes(mpx, m, two)
        for copy in x_copies:
            copy.arrived()
        vz[k, iz] = prefixes(vx, k, lambda q: load_halves(gx, q), 0, ix)
        z_copies = exchange(vz, k, iz, on_z)
        if k == 0:
            pass_on(gz, iz, z_matrices)
            m, two, total = products(gz, mpz)
            store_halves(gy, iy, total)
            y_matrices = send_matrix(gy, iy, on_y, y_matrix_conditions)
            store_prefixes(mpz, m, two)
        for copy in z_copies:
            copy.arrived()
        vy[k, iy] = prefixes(vz, k, lambda q: load_halves(gz, q), 1, iz)
        y_copies = exchange(vy, k, iy, on_y, y_conditions)
        top_copy.arrived()
        after_top = next_top[k]
        offset = bottom_block - times_exact(after_top, up[:, last])
        if k == 0:
            low_copy.arrived()
            pass_on(gy, iy, y_matrices)
        for copy in y_copies:
            copy.arrived()
        prefixes(vy, k, lambda q: load_halves(gy, q), 2, iy, total=False)
        carried = prefix[2, iy]
        carried = prefix[1, iz] + times_pair(carried, mpz[iz, :BAND, :], mpz[iz, BAND:, :])
        carried = prefix[0, ix] + times_pair(carried, mpx[ix, :BAND, :], mpx[ix, BAND:, :])
        second = vc[k, 0] - times_exact(carried, pair_mat[0])
        carried = jnp.where(core == 0, carried, second)
        previous = carried + shift
        current = offset - times_exact(previous, pair_mat[core])
        top = after_top - times_exact(current, low_after[...])
        top_rounded, previous_rounded = rounded(top), rounded(previous)
        for m in (0, 3, 1, 2):
            cols = slice(m * BAND, (m + 1) * BAND)
            own = slice((m + 1) * BAND, (m + 2) * BAND)
            block = bottom_block if m == 3 else local[k, :, cols]
            block = block - dot(top_rounded, up[:, cols])
            block = block - dot(previous_rounded, low[:, cols])
            new = xp[k, :, own] + block
            xp[k + 1, :, own] = new
            if k == ITERS - 1:
                x_out[:, cols] = new
            if m == 3:
                edges = send_edges(k + 1)

    residual(ITERS, edges)
    ones = jnp.ones((8, 128), F32)
    contract = (((1,), (1,)), ((), ()))
    totals[3, 0] = jnp.zeros((8, 128), F32)
    for k in range(ITERS + 1):
        row = lax.dot_general(
            ones, squares[k], contract, precision=lax.Precision.HIGHEST, preferred_element_type=F32
        )
        totals[3, 0, k : k + 1, :RHS] = row[:1, :]

    totals[0, core] = totals[3, 0]
    copy = Copy(totals.at[0, core], totals.at[0, core], partner)
    copy.arrived()
    value = totals[0, 0] + totals[0, 1]
    for level, (slot, peer_of) in enumerate(((ix, on_x), (iz, on_z), (iy, on_y))):
        ref = totals if level == 0 else None
        totals[4 + level, slot] = value
        copies = [
            Copy(totals.at[4 + level, slot], totals.at[4 + level, slot], peer_of(d))
            for d in (1, 2, 3)
        ]
        for copy in copies:
            copy.arrived()
        value = (totals[4 + level, 0] + totals[4 + level, 1]) + (
            totals[4 + level, 2] + totals[4 + level, 3]
        )
    norm_out[...] = jnp.sqrt(value * (1.0 / ORDER))
    for copy in sent:
        copy.left()


def body(*args):
    any_space = pl.BlockSpec(memory_space=pl.ANY)
    vmem = pl.BlockSpec(memory_space=pltpu.VMEM)
    matrix4 = pltpu.VMEM((4, 2, BAND, BAND), BF16)
    prefix4 = pltpu.VMEM((4, 2 * BAND, BAND), BF16)
    vectors4 = pltpu.VMEM((ITERS, 4, RHS, BAND), F32)
    x, norms = pl.pallas_call(
        kernel,
        out_shape=(
            jax.ShapeDtypeStruct((RHS, COLS), F32),
            jax.ShapeDtypeStruct((8, 128), F32),
        ),
        in_specs=[any_space] * 8,
        out_specs=(vmem, vmem),
        scratch_shapes=[
            pltpu.VMEM((RHS, COLS), F32),
            pltpu.VMEM((COLS, BAND), F32),
            pltpu.VMEM((COLS, BAND), F32),
            pltpu.VMEM((COLS, BAND), F32),
            pltpu.VMEM((COLS, COLS), BF16),
            pltpu.VMEM((BAND, COLS), BF16),
            pltpu.VMEM((BAND, COLS), BF16),
            pltpu.VMEM((4, 3 * BAND, BAND), BF16),
            pltpu.VMEM((4, 3 * BAND, BAND), BF16),
            pltpu.VMEM((ITERS + 1, RHS, COLS + 2 * BAND), F32),
            pltpu.VMEM((2, BAND, BAND), BF16),
            pltpu.VMEM((BAND, BAND), BF16),
            pltpu.VMEM((BAND, BAND), BF16),
            matrix4,
            matrix4,
            matrix4,
            prefix4,
            prefix4,
            pltpu.VMEM((ITERS, RHS, COLS), F32),
            pltpu.VMEM((ITERS, RHS, BAND), F32),
            pltpu.VMEM((ITERS, 2, RHS, BAND), F32),
            vectors4,
            vectors4,
            vectors4,
            pltpu.VMEM((3, 4, RHS, BAND), F32),
            pltpu.VMEM((ITERS + 1, RHS, 128), F32),
            pltpu.VMEM((7, 4, 8, 128), F32),
            pltpu.SemaphoreType.DMA((16,)),
            pltpu.SemaphoreType.DMA((COPIES,)),
            pltpu.SemaphoreType.DMA((COPIES,)),
        ],
        compiler_params=pltpu.CompilerParams(collective_id=0, has_side_effects=True),
    )(*args)
    return x, norms[: ITERS + 1, :RHS]


def solution(mesh):
    cols, rows = P(None, "rows"), P("rows", None)
    return jax.shard_map(
        body,
        mesh=mesh,
        in_specs=(cols, cols, rows, rows, rows, rows, cols, cols),
        out_specs=(cols, P()),
        check_vma=False,
    )
```

time: 261 us -> 78.3 us (0.30)
  blocking collectives: 125 us -> 0 us
  Pallas kernels: 0 us -> 74.7 us
  matrix products: 55.2 us -> 0 us
  waiting for transfers between devices: 26.6 us -> 0 us
  local copies, waits for them, and re-layouts: 19 us -> 2.83 us
  between operations: 14.9 us -> 0.64 us
  starting transfers between devices: 12.8 us -> 0 us
  other arithmetic: 4.58 us -> 0 us
    all_gather x9 -> x0, blocking collectives: 92.3 us -> none  [prefix_by_axis(): pieces = jax.tree.map(lambda part: lax.all_gather(part, axis), running)]
    pallas_call x0 -> x1, Pallas kernels: none -> 74.7 us  [body(): pl.pallas_call(kernel, out_shape=(jax.ShapeDtypeStruct((RHS, COLS), F32),...]
    dot_general x66 -> x0, matrix products: 55.2 us -> none  [the longest x32 26.2 us: compose(): jnp.matmul(earlier[1], successor_block[0], precision=maximum_level)]
    psum x4 -> x0, blocking collectives: 32.9 us -> none  [one_axis_at_a_time(): return functools.reduce(lax.psum, axes, value)]
    all_gather x3 -> x0, waiting for transfers between devices: 16 us -> none  [prefix_by_axis(): pieces = jax.tree.map(lambda part: lax.all_gather(part, axis), running)]
    ppermute x9 -> x0, starting transfers between devices: 12.6 us -> none  [the longest x3 4.62 us: with_halo(): lax.ppermute(lax.slice_in_dim(block, block.shape[dim] - width, None, axis...]
    ppermute x9 -> x0, waiting for transfers between devices: 10.6 us -> none  [the longest x3 6.69 us: with_halo(): lax.ppermute(lax.slice_in_dim(block, 0, width, axis=dim), axis, backward)]
    unnamed x116 -> x1, local copies, waits for them, and re-layouts: 8.11 us -> 1.57 us
  transfers between devices with their start and end apart: 12 -> 0, of which waited for: 4 -> 0; matrix products, arithmetic and copies ran while one was open for 20% -> 0% of each run, Pallas kernels for 0% -> 0%
where the time goes in v1:
time: 78.3 us; the launch traced here: 78.2 us
  Pallas kernels  74.7 us (95%)
  local copies, waits for them, and re-layouts  2.83 us (4%)
    pallas_call x1, Pallas kernels, body(): pl.pallas_call(kernel, out_shape=(jax.ShapeDtypeStruct((RHS, COLS), F32),...  74.7 us
    unnamed x1, local copies, waits for them, and re-layouts  1.57 us

profile of v1, /device:TPU:0, one launch (start us, length us, event | category | flops | bytes accessed | tf_op | source)
XLA Modules:
  0.0 78.2 jit_solution(16800616955375996713)
XLA Ops:
  0.6 74.7 %shard_map.95 = (f32[32,1024]{1,0:T(8,128)}, f32[8,128]{1,0:T(8,128)}) custom-call(f32[32,1024]{1,0:T(8,128)} %rhs_hbm.1, f32[32,1024]{1,0:T(8,128)} %x0_hbm.1, f32[1024,256]{1,0:T(8,128)} %diag_hbm.1, f32[1024,256]{1,0:T(8,128)} %sub_hbm.1, f32[1024,256]{1,0:T(8,128)} %sup_hbm.1, bf16[1024,1024]{1,0:T(8,128)(2,1)} %inv_hbm.1, bf16[256,1024]{1,0:T(8,128)(2,1)} %up_hbm.1, ...), custom_call_target="tpu_custom_call" | custom-call | tf_op jit(solution)/shard_map/pallas_call | solution.py:411
  75.4 1.3 %slice.3 = f32[3,32]{1,0:T(4,128)} slice(f32[8,128]{1,0:T(8,128)} %get-tuple-element.5), slice={[0:3], [0:32]} | slice | bytes 768 | tf_op jit(solution)/shard_map/slice | solution.py:453
  76.6 1.6 %copy.11 = f32[32,1024]{1,0:T(8,128)} copy(f32[32,1024]{1,0:T(8,128)} %get-tuple-element.8) | data formatting | bytes 262144
